TPU v7x, 32 devices: a whole 2x2x4 slice. The times are simulated.
32 devices in a mesh: groups: 2 (over x), seq: 16 (over z, y, core).
Axes of the slice: x: 2, y: 2, z: 4, core: 2. Of those that a mesh axis runs over, the one named last changes fastest.
Arguments:
- hidden_in: bfloat16 [32768, 2048], P(('groups', 'seq')), parts along dimension 0, may hold values from -6 to 6
- queries: bfloat16 [32768, 1024], P(('groups', 'seq')), parts along dimension 0, may hold values from -6 to 6
- kv_weight: bfloat16 [2048, 2048], replicated, may hold values from -0.125 to 0.125
- level_weight: float32 [16, 8], replicated, may hold values from 0.3 to 3
Outputs:
- attended: bfloat16 [32768, 1024], P(('groups', 'seq')), parts along dimension 0
There are 2 independent parts, one for each index of `groups`. A program takes and returns all parts, laid end to end along the dimension named above; an argument that names none is the same for every part. Nothing has to cross between parts.
All inputs are finite; a program needn't handle non-finite values.
Results may differ from a plain program's by a relative error of at most 0.0034.
Values sent between devices are 32-bit elements; how exact they have to be, the bound alone decides.
A program may use at most 128 MiB of HBM per device.

v0:
```python
import jax
import jax.numpy as jnp
from jax import lax
from jax.sharding import PartitionSpec as P

HEADS = 8
HEAD = 128
SPAN = 64


def swapped(x, axis, distance):
    return lax.ppermute(x, axis, [(i, i ^ 1 << distance) for i in range(lax.axis_size(axis))])


def in_span(query_blocks, keys, values, level_weight):
    causal = jnp.tril(jnp.ones((SPAN, SPAN), jnp.float32))
    diag_scale = level_weight[0] / jnp.sqrt(jnp.float32(SPAN * HEAD))
    scores = jnp.einsum("jtha,jsha->jhts", query_blocks, keys, preferred_element_type=jnp.float32)
    scores = (scores * diag_scale[None, :, None, None] * causal[None, None]).astype(jnp.bfloat16)
    return jnp.einsum("jhts,jshb->jthb", scores, values, preferred_element_type=jnp.float32)


def remote_states(total, level_weight, local_bits, tokens):
    index = lax.axis_index("seq")
    depth = lax.axis_size("seq").bit_length() - 1
    remote = jnp.zeros_like(total)
    block = total
    for level in range(depth):
        bit = jnp.right_shift(index, level) & 1
        partner = swapped(block, "seq", level)
        factor = level_weight[1 + local_bits + level] / jnp.sqrt(jnp.float32(2**level * tokens))
        remote = remote + bit.astype(jnp.float32) * factor[:, None, None] * partner
        block = block + partner
    return remote


def local(hidden_in, queries, kv_weight, level_weight):
    tokens = hidden_in.shape[0]
    width = HEADS * HEAD
    count = tokens // SPAN
    local_bits = count.bit_length() - 1
    highest = lax.Precision.HIGHEST
    kv = jnp.dot(hidden_in, kv_weight, preferred_element_type=jnp.float32).astype(jnp.bfloat16)
    keys = kv[:, :width].reshape(count, SPAN, HEADS, HEAD)
    values = kv[:, width:].reshape(count, SPAN, HEADS, HEAD)
    query_blocks = queries.reshape(count, SPAN, HEADS, HEAD)
    span_states = jnp.einsum("jcha,jchb->jhab", keys, values, preferred_element_type=jnp.float32)
    total = jnp.sum(span_states, axis=0)
    remote = remote_states(total, level_weight, local_bits, tokens)
    intra = in_span(query_blocks, keys, values, level_weight)
    target = jnp.arange(count, dtype=jnp.int32)[:, None]
    source = jnp.arange(count, dtype=jnp.int32)[None, :]
    coef = jnp.zeros((count, count, HEADS), jnp.float32)
    for level in range(local_bits):
        member = jnp.right_shift(target, level) & 1 == 1
        member = member & (jnp.right_shift(source, level + 1) == jnp.right_shift(target, level + 1))
        member = member & (jnp.right_shift(source, level) & 1 == 0)
        factor = level_weight[1 + level] / jnp.sqrt(jnp.float32(2**level * SPAN))
        coef = coef + member.astype(jnp.float32)[:, :, None] * factor[None, None, :]
    local_states = jnp.einsum("jih,ihab->jhab", coef, span_states, precision=highest)
    states = local_states + remote[None]
    inter = jnp.einsum(
        "jtha,jhab->jthb", query_blocks.astype(jnp.float32), states, precision=highest
    )
    inter = inter / jnp.sqrt(jnp.float32(HEAD))
    return (intra + inter).astype(jnp.bfloat16).reshape(tokens, width)


def solution(mesh):
    in_specs = (P(("groups", "seq"), None), P(("groups", "seq"), None), P(), P())
    out_specs = P(("groups", "seq"), None)
    return jax.shard_map(local, mesh=mesh, in_specs=in_specs, out_specs=out_specs, check_vma=False)
```

profile of v0, /device:TPU:0, one launch (start us, length us, event | category | flops | bytes accessed | tf_op | source)
XLA Modules:
  0.0 98.0 jit_solution(12695792420870214556)
XLA Ops:
  0.0 12.5 %convolution_convert_fusion = bf16[1024,2048]{1,0:T(8,128)(2,1)S(1)} fusion(bf16[1024,2048]{1,0:T(8,128)(2,1)} %param.4, bf16[2048,2048]{1,0:T(8,128)(2,1)} %param.6), kind=kOutput, calls=%fused_computation.9 | convolution fusion | flops 8592031744 | bytes 16777216 | tf_op jit(solution)/shard_map/dot_general | solution.py:43
  12.5 1.2 %slice_bitcast_fusion.1 = (bf16[128,8,8,128]{3,1,2,0:T(8,128)(2,1)S(1)}, bf16[128,8,8,128]{3,1,2,0:T(8,128)(2,1)S(1)}) fusion(bf16[1024,2048]{1,0:T(8,128)(2,1)S(1)} %convolution_convert_fusion), kind=kLoop, calls=%fused_computation.13 | loop fusion | bytes 8388608
  13.7 0.6 copy.19
  14.3 0.6 copy.17
  14.9 0.0 copy-start
  14.9 0.0 copy-start.2
  15.0 4.7 %fusion.24 = (f32[8,128,128]{2,1,0:T(8,128)S(1)}, f32[16,8,128,128]{3,2,1,0:T(8,128)}) fusion(bf16[16,64,8,128]{3,2,1,0:T(8,128)(2,1)S(1)} %bitcast.34, bf16[16,64,8,128]{3,2,1,0:T(8,128)(2,1)S(1)} %bitcast.36), kind=kOutput, calls=%fused_computation.52 | convolution fusion | flops 270401536 | bytes 13107200 | tf_op jit(solution)/shard_map/jcha,jchb->jhab/dot_general | solution.py:47
  19.6 0.5 collective-permute-start
  20.2 0.1 and_convert_fusion
  20.3 0.3 multiply_reduce_fusion.3
  20.6 0.1 and_convert_fusion.1
  20.7 0.1 and_convert_fusion.2
  20.8 1.0 %collective-permute-done = f32[8,128,128]{2,1,0:T(8,128)} collective-permute-done((f32[8,128,128]{2,1,0:T(8,128)S(1)}, f32[8,128,128]{2,1,0:T(8,128)}, u32[]{:S(2)}, u32[]{:S(2)}) %collective-permute-start) | collective-permute-done | bytes 524320 | tf_op jit(solution)/shard_map/ppermute | solution.py:12
  21.8 1.1 %add.45 = f32[8,128,128]{2,1,0:T(8,128)S(1)} add(f32[8,128,128]{2,1,0:T(8,128)S(1)} %get-tuple-element.16, f32[8,128,128]{2,1,0:T(8,128)} %collective-permute-done) | non-fusion elementwise | flops 131072 | bytes 1572864 | tf_op jit(solution)/shard_map/add | solution.py:33
  22.9 2.9 %collective-permute-start.1 = (f32[8,128,128]{2,1,0:T(8,128)S(1)}, f32[8,128,128]{2,1,0:T(8,128)S(1)}, u32[]{:S(2)}, u32[]{:S(2)}) collective-permute-start(f32[8,128,128]{2,1,0:T(8,128)S(1)} %add.45), channel_id=1, source_target_pairs={{0,2},{1,3},{2,0},{3,1},{4,6},{5,7},{6,4},{7,5},{8,10},{9,11},{10,... | collective-permute-start | bytes 1572872 | tf_op jit(solution)/shard_map/ppermute | solution.py:12
  25.8 0.1 and_convert_fusion.3
  25.9 0.2 add_bitcast_fusion
  26.1 0.1 copy.15
  26.2 3.5 %copy.18 = bf16[128,8,8,128]{3,2,1,0:T(8,128)(2,1)} copy(bf16[128,8,8,128]{3,1,2,0:T(8,128)(2,1)} %bitcast.41) | data formatting | bytes 4194304
  29.8 8.3 %collective-permute-done.1 = f32[8,128,128]{2,1,0:T(8,128)S(1)} collective-permute-done((f32[8,128,128]{2,1,0:T(8,128)S(1)}, f32[8,128,128]{2,1,0:T(8,128)S(1)}, u32[]{:S(2)}, u32[]{:S(2)}) %collective-permute-start.1) | collective-permute-done | bytes 524320 | tf_op jit(solution)/shard_map/ppermute | solution.py:12
  38.0 0.1 add.47
  38.1 1.9 %collective-permute-start.2 = (f32[8,128,128]{2,1,0:T(8,128)S(1)}, f32[8,128,128]{2,1,0:T(8,128)S(1)}, u32[]{:S(2)}, u32[]{:S(2)}) collective-permute-start(f32[8,128,128]{2,1,0:T(8,128)S(1)} %add.47), channel_id=1, source_target_pairs={{0,4},{1,5},{2,6},{3,7},{4,0},{5,1},{6,2},{7,3},{8,12},{9,13},{10,... | collective-permute-start | bytes 1572872 | tf_op jit(solution)/shard_map/ppermute | solution.py:12
  40.0 17.0 %fusion.2 = f32[8,128,128,16]{2,3,1,0:T(8,128)} fusion(f32[16,16,8,1]{0,1,3,2:T(8,128)S(1)} %copy.15, f32[16,8,128,128]{3,2,1,0:T(8,128)} %get-tuple-element.17), kind=kOutput, calls=%fused_computation.3 | convolution fusion | flops 402653184 | bytes 16785408 | tf_op jit(solution)/shard_map/jih,ihab->jhab/dot_general | solution.py:60
  57.0 0.0 collective-permute-done.2
  57.0 0.9 add.49
  57.9 2.6 %collective-permute-start.3 = (f32[8,128,128]{2,1,0:T(8,128)}, f32[8,128,128]{2,1,0:T(8,128)}, u32[]{:S(2)}, u32[]{:S(2)}) collective-permute-start(f32[8,128,128]{2,1,0:T(8,128)} %add.49), channel_id=1, source_target_pairs={{0,8},{1,9},{2,10},{3,11},{4,12},{5,13},{6,14},{7,15},{8,0},{9,1},... | collective-permute-start | bytes 1572872 | tf_op jit(solution)/shard_map/ppermute | solution.py:12
  60.5 6.0 %fusion.15 = f32[16,8,128,64]{2,3,1,0:T(8,128)} fusion(bf16[16,64,8,128]{3,2,1,0:T(8,128)(2,1)S(1)} %bitcast.35, f32[64,64]{1,0:T(8,128)S(1)} %fusion.21, f32[8]{0:T(128)S(1)} %get-tuple-element.11, bf16[16,64,8,128]{3,2,1,0:T(8,128)(2,1)} %bitcast.38, bf16[16,64,8,128]{3,2,1,0:T(8,128)(2,1)} %bitcast.37), kind=kOutput, calls=%fused_computation.20 | convolution fusion | flops 270008320 | bytes 10502176 | tf_op jit(solution)/shard_map/jhts,jshb->jthb/dot_general | solution.py:20
  66.5 16.6 %collective-permute-done.3 = f32[8,128,128]{2,1,0:T(8,128)} collective-permute-done((f32[8,128,128]{2,1,0:T(8,128)}, f32[8,128,128]{2,1,0:T(8,128)}, u32[]{:S(2)}, u32[]{:S(2)}) %collective-permute-start.3) | collective-permute-done | bytes 524320 | tf_op jit(solution)/shard_map/ppermute | solution.py:12
  83.1 1.4 %multiply_add_fusion = f32[8,128,128]{2,1,0:T(8,128)S(1)} fusion(f32[8,128,128]{2,1,0:T(8,128)} %collective-permute-done.3, f32[8,128,128]{2,1,0:T(8,128)S(1)} %collective-permute-done.2, f32[8,128,128]{2,1,0:T(8,128)S(1)} %collective-permute-done.1, f32[8,128,128]{2,1,0:T(8,128)} %collective-permute-done, f32[8]{0:T(128)S(1)} %get-tuple-element.12, ...), kind=kLoop, calls=%fused_computation.22 | loop fusion | flops 917504 | bytes 2621568 | tf_op jit(solution)/shard_map/add | solution.py:32
  84.6 9.7 %fusion.6 = bf16[16,64,8,128]{3,1,2,0:T(8,128)(2,1)S(1)} fusion(f32[16,8,128,64]{2,3,1,0:T(8,128)} %fusion.15, f32[8,128,128,16]{2,3,1,0:T(8,128)} %fusion.2, f32[8,128,128]{2,1,0:T(8,128)S(1)} %multiply_add_fusion, bf16[16,64,8,128]{3,2,1,0:T(8,128)(2,1)S(1)} %bitcast.39), kind=kOutput, calls=%fused_computation.10 | convolution fusion | flops 1615855616 | bytes 17301504 | tf_op jit(solution)/shard_map/jtha,jhab->jthb/dot_general | solution.py:62
  94.3 1.8 %copy.13 = bf16[16,64,8,128]{3,2,1,0:T(8,128)(2,1)S(1)} copy(bf16[16,64,8,128]{3,1,2,0:T(8,128)(2,1)S(1)} %fusion.6) | data formatting | bytes 4194304 | tf_op jit(solution)/shard_map/convert_element_type | solution.py:66
  96.1 2.0 %copy.50 = bf16[128,8,8,128]{3,1,2,0:T(8,128)(2,1)} copy(bf16[128,8,8,128]{3,2,1,0:T(8,128)(2,1)S(1)} %bitcast.40) | data formatting | bytes 4194304
  (13 shorter events, 0.1 us)
Async XLA Ops:
  14.9 4.7 %copy-start = (bf16[128,8,8,128]{3,2,1,0:T(8,128)(2,1)}, bf16[128,8,8,128]{3,2,1,0:T(8,128)(2,1)S(1)}, u32[]{:S(2)}) copy-start(bf16[128,8,8,128]{3,2,1,0:T(8,128)(2,1)S(1)} %copy.17) | copy-start | bytes 6291460
  14.9 5.3 %copy-start.2 = (f32[16,8]{0,1:T(8,128)S(1)}, f32[16,8]{0,1:T(8,128)}, u32[]{:S(2)}) copy-start(f32[16,8]{0,1:T(8,128)} %param.7) | copy-start | bytes 1540
  19.6 2.2 %collective-permute-start = (f32[8,128,128]{2,1,0:T(8,128)S(1)}, f32[8,128,128]{2,1,0:T(8,128)}, u32[]{:S(2)}, u32[]{:S(2)}) collective-permute-start(f32[8,128,128]{2,1,0:T(8,128)S(1)} %get-tuple-element.16), channel_id=1, source_target_pairs={{0,1},{1,0},{2,3},{3,2},{4,5},{5,4},{6,7},{7,6},{8,9},{9,8},{10,11... | collective-permute-start | bytes 1572872 | tf_op jit(solution)/shard_map/ppermute | solution.py:12
  22.9 15.2 %collective-permute-start.1 = (f32[8,128,128]{2,1,0:T(8,128)S(1)}, f32[8,128,128]{2,1,0:T(8,128)S(1)}, u32[]{:S(2)}, u32[]{:S(2)}) collective-permute-start(f32[8,128,128]{2,1,0:T(8,128)S(1)} %add.45), channel_id=1, source_target_pairs={{0,2},{1,3},{2,0},{3,1},{4,6},{5,7},{6,4},{7,5},{8,10},{9,11},{10,... | collective-permute-start | bytes 1572872 | tf_op jit(solution)/shard_map/ppermute | solution.py:12
  38.1 18.9 %collective-permute-start.2 = (f32[8,128,128]{2,1,0:T(8,128)S(1)}, f32[8,128,128]{2,1,0:T(8,128)S(1)}, u32[]{:S(2)}, u32[]{:S(2)}) collective-permute-start(f32[8,128,128]{2,1,0:T(8,128)S(1)} %add.47), channel_id=1, source_target_pairs={{0,4},{1,5},{2,6},{3,7},{4,0},{5,1},{6,2},{7,3},{8,12},{9,13},{10,... | collective-permute-start | bytes 1572872 | tf_op jit(solution)/shard_map/ppermute | solution.py:12
  57.9 25.2 %collective-permute-start.3 = (f32[8,128,128]{2,1,0:T(8,128)}, f32[8,128,128]{2,1,0:T(8,128)}, u32[]{:S(2)}, u32[]{:S(2)}) collective-permute-start(f32[8,128,128]{2,1,0:T(8,128)} %add.49), channel_id=1, source_target_pairs={{0,8},{1,9},{2,10},{3,11},{4,12},{5,13},{6,14},{7,15},{8,0},{9,1},... | collective-permute-start | bytes 1572872 | tf_op jit(solution)/shard_map/ppermute | solution.py:12
  66.5 18.1 %copy-start.1 = (bf16[128,8,8,128]{3,2,1,0:T(8,128)(2,1)S(1)}, bf16[128,8,8,128]{3,2,1,0:T(8,128)(2,1)}, u32[]{:S(2)}) copy-start(bf16[128,8,8,128]{3,2,1,0:T(8,128)(2,1)} %copy.18) | copy-start | bytes 6291460
where the time goes:
time: 98.2 us; the launch traced here: 98 us
  matrix products  49.8 us (51%)
  waiting for transfers between devices  25.9 us (26%)
  local copies, waits for them, and re-layouts  9.83 us (10%)
  starting transfers between devices  7.88 us (8%)
  other arithmetic  4.38 us (4%)
    ppermute x4, waiting for transfers between devices, swapped(): lax.ppermute(x, axis, [(i, i ^ 1 << distance) for i in range(lax.axis_siz...  25.9 us
    dot_general x1, matrix products, local(): jnp.einsum('jih,ihab->jhab', coef, span_states, precision=highest)  17 us
    dot_general x1, matrix products, local(): jnp.dot(hidden_in, kv_weight, preferred_element_type=jnp.float32)  12.5 us
    dot_general x1, matrix products, local(): jnp.einsum('jtha,jhab->jthb', query_blocks.astype(jnp.float32), states, p...  9.69 us
    unnamed x11, local copies, waits for them, and re-layouts  7.94 us
    ppermute x4, starting transfers between devices, swapped(): lax.ppermute(x, axis, [(i, i ^ 1 << distance) for i in range(lax.axis_siz...  7.88 us
    dot_general x1, matrix products, in_span(): jnp.einsum('jhts,jshb->jthb', scores, values, preferred_element_type=jnp....  6 us
    dot_general x1, matrix products, local(): jnp.einsum('jcha,jchb->jhab', keys, values, preferred_element_type=jnp.fl...  4.66 us
  transfers between devices with their start and end apart: 4, of which 3 were waited for; matrix products, arithmetic and copies ran while one was open for 28% of the time, Pallas kernels for 0%

commit v1 on v0

v1 whole, which is shorter than its diff:
```python
import functools
import math

import jax
import jax.numpy as jnp
from jax import lax
from jax.experimental import pallas as pl
from jax.experimental.pallas import tpu as pltpu
from jax.sharding import PartitionSpec as P

HEADS = 8
HEAD = 128
SPAN = 64
PAIR = 2
MESH = pl.DeviceIdType.MESH
F32 = jnp.float32
BF16 = jnp.bfloat16


def kernel(depth, tokens, block, tile, x_hbm, q_hbm, w_hbm, lw, out_hbm,
           x, w, q, kv, local, out, weight, states, total, near, away, sums, got,
           x_sem, w_sem, q_sem, out_sem, near_send, near_recv, far_send, far_recv, share_send, share_recv):
    width = HEADS * HEAD
    wide = PAIR * HEAD
    groups = HEADS // PAIR
    blocks = tokens // block
    tiles = tokens // tile
    inner_bits = (block // SPAN).bit_length() - 1
    local_bits = (tokens // SPAN).bit_length() - 1
    index = lax.axis_index("seq")
    core = index & 1
    partners = [index ^ (1 << level) for level in range(depth)]

    barrier = pltpu.get_barrier_semaphore()
    for partner in partners:
        pl.semaphore_signal(barrier, inc=1, device_id={"seq": partner}, device_id_type=MESH)

    def x_copy(i):
        rows = pl.ds(i * tile, tile)
        return pltpu.make_async_copy(x_hbm.at[rows], x.at[rows], x_sem.at[i])

    def w_copy(g, side):
        columns = pl.ds(side * width + g * wide, wide)
        return pltpu.make_async_copy(w_hbm.at[:, columns], w.at[g, side], w_sem.at[g, side])

    q_copy = pltpu.make_async_copy(q_hbm, q, q_sem)

    def out_copy(g):
        columns = pl.ds(g * wide, wide)
        return pltpu.make_async_copy(out.at[:, columns], out_hbm.at[:, columns], out_sem.at[g])

    w_copy(0, 0).start()
    x_copy(0).start()
    w_copy(0, 1).start()
    for i in range(1, tiles):
        x_copy(i).start()
    for g in range(1, groups):
        w_copy(g, 0).start()
        w_copy(g, 1).start()
    q_copy.start()

    def remote(src, dst, send, recv, partner):
        return pltpu.make_async_remote_copy(
            src_ref=src, dst_ref=dst, send_sem=send, recv_sem=recv,
            device_id={"seq": partner}, device_id_type=MESH)

    def near_copy(g):
        return remote(total.at[g], near.at[g], near_send.at[g], near_recv.at[g], partners[0])

    def far_copy(g, level):
        return remote(sums.at[level - 1, g], got.at[level - 1, g], far_send.at[level - 1, g],
                      far_recv.at[level - 1, g], partners[level])

    def share_copy(g):
        return remote(away.at[g, core], away.at[g, core], share_send.at[g], share_recv.at[g], partners[0])

    def factor(level, head):
        return lw[1 + level, head] * (1.0 / math.sqrt(2**level * SPAN))

    def project(g):
        kc = slice(g * wide, (g + 1) * wide)
        vc = slice(width + g * wide, width + (g + 1) * wide)
        w_copy(g, 0).wait()
        w_copy(g, 1).wait()

        def body(i):
            rows = pl.ds(pl.multiple_of(i * tile, tile), tile)
            xt = x[rows, :]
            keys = jnp.dot(xt, w[g, 0], preferred_element_type=F32).astype(BF16)
            values = jnp.dot(xt, w[g, 1], preferred_element_type=F32).astype(BF16)
            kv[rows, kc] = keys
            kv[rows, vc] = values
            for b in range(tile // block):
                part = slice(b * block, (b + 1) * block)
                both = lax.dot_general(keys[part], values[part], (((0,), (0,)), ((), ())),
                                       preferred_element_type=F32)
                for e in range(PAIR):
                    own = slice(e * HEAD, (e + 1) * HEAD)
                    states[g * PAIR + e, i * (tile // block) + b] = both[own, own]

        if g == 0:
            for i in range(tiles):
                x_copy(i).wait()
                body(i)
        else:
            pl.loop(0, tiles)(body)
        for e in range(PAIR):
            total[g, e] = sum(states[g * PAIR + e, b] for b in range(blocks))

    def attend(g):
        if g == 0:
            q_copy.wait()
        target = lax.broadcasted_iota(jnp.int32, (block, block), 0)
        source = lax.broadcasted_iota(jnp.int32, (block, block), 1)
        differ = (target // SPAN) ^ (source // SPAN)
        for e in range(PAIR):
            head = g * PAIR + e
            at = jnp.full((block, block), lw[0, head] * (1.0 / math.sqrt(SPAN * HEAD)), F32)
            for level in range(inner_bits):
                at = jnp.where(differ >= 1 << level, factor(level, head) * (1.0 / math.sqrt(HEAD)), at)
            weight[e] = jnp.where(source <= target, at, 0.0)

        @pl.loop(0, blocks)
        def _(b):
            rows = pl.ds(pl.multiple_of(b * block, block), block)
            for e in range(PAIR):
                head = g * PAIR + e
                columns = slice(head * HEAD, (head + 1) * HEAD)
                keys = kv[rows, columns]
                values = kv[rows, width + head * HEAD:width + (head + 1) * HEAD]
                scores = lax.dot_general(q[rows, columns], keys, (((1,), (1,)), ((), ())),
                                         preferred_element_type=F32)
                scores = (scores * weight[e]).astype(BF16)
                local[rows, columns] = jnp.dot(scores, values, preferred_element_type=F32)

    def finish(g):
        for e in range(PAIR):
            head = g * PAIR + e
            columns = slice(head * HEAD, (head + 1) * HEAD)
            bit = core.astype(F32) * factor(local_bits, head)
            base = away[g, e] + bit * near[g, e]
            for b in range(blocks):
                mixed = base
                for level in range(local_bits - inner_bits):
                    if b >> level & 1:
                        first = (b >> level + 1) << level + 1
                        held = sum(states[head, j] for j in range(first, first + (1 << level)))
                        mixed = mixed + factor(inner_bits + level, head) * held
                mixed = mixed * (1.0 / math.sqrt(HEAD))
                high = mixed.astype(BF16)
                low = (mixed - high.astype(F32)).astype(BF16)
                rows = slice(b * block, (b + 1) * block)
                qb = q[rows, columns]
                inter = jnp.dot(jnp.concatenate([qb, qb], 1), jnp.concatenate([high, low], 0),
                                preferred_element_type=F32)
                out[rows, columns] = (local[rows, columns] + inter).astype(BF16)
        out_copy(g).start()

    def stage(g, s):
        if s == 0:
            if g == 0:
                pl.semaphore_wait(barrier, depth)
            near_copy(g).start()
        elif s == 1:
            near_copy(g).wait()
            if depth > 1:
                sums[0, g] = total[g, core] + near[g, core]
                far_copy(g, 1).start()
        elif s <= depth:
            level = s - 1
            far_copy(g, level).wait()
            bit = (jnp.right_shift(index, level) & 1).astype(F32)
            term = (bit * factor(local_bits + level, g * PAIR + core)) * got[level - 1, g]
            away[g, core] = term if level == 1 else away[g, core] + term
            if level + 1 < depth:
                sums[level, g] = sums[level - 1, g] + got[level - 1, g]
                far_copy(g, level + 1).start()
            else:
                share_copy(g).start()
        else:
            share_copy(g).wait()
            finish(g)

    for slot in range(2 * groups + depth + 1):
        if slot < groups:
            project(slot)
        elif slot < 2 * groups:
            attend(slot - groups)
        for g in range(groups):
            lag = slot - g
            if slot >= groups and g == groups - 1:
                lag = slot - g
            if 0 <= lag <= depth:
                stage(g, lag)
            if slot >= 2 * groups - 1 and lag == max(depth + 1, 2 * groups - 1 - g):
                stage(g, depth + 1)
    for g in range(groups):
        out_copy(g).wait()


def local(depth, x, q, w, lw):
    tokens, width = q.shape
    groups = HEADS // PAIR
    block = min(256, tokens)
    tile = min(512, tokens)
    levels = max(depth - 1, 1)
    dma = pltpu.SemaphoreType.DMA
    hbm = pl.BlockSpec(memory_space=pl.ANY)
    return pl.pallas_call(
        functools.partial(kernel, depth, tokens, block, tile),
        out_shape=jax.ShapeDtypeStruct((tokens, width), BF16),
        in_specs=[hbm, hbm, hbm, pl.BlockSpec(memory_space=pltpu.SMEM)],
        out_specs=hbm,
        scratch_shapes=[
            pltpu.VMEM(x.shape, BF16),
            pltpu.VMEM((groups, 2, w.shape[0], PAIR * HEAD), BF16),
            pltpu.VMEM(q.shape, BF16),
            pltpu.VMEM((tokens, 2 * width), BF16),
            pltpu.VMEM((tokens, width), F32),
            pltpu.VMEM((tokens, width), BF16),
            pltpu.VMEM((PAIR, block, block), F32),
            pltpu.VMEM((HEADS, tokens // block, HEAD, HEAD), F32),
            pltpu.VMEM((groups, PAIR, HEAD, HEAD), F32),
            pltpu.VMEM((groups, PAIR, HEAD, HEAD), F32),
            pltpu.VMEM((groups, PAIR, HEAD, HEAD), F32),
            pltpu.VMEM((levels, groups, HEAD, HEAD), F32),
            pltpu.VMEM((levels, groups, HEAD, HEAD), F32),
            dma((tokens // tile,)), dma((groups, 2)), dma, dma((groups,)),
            dma((groups,)), dma((groups,)), dma((levels, groups)), dma((levels, groups)),
            dma((groups,)), dma((groups,)),
        ],
        compiler_params=pltpu.CompilerParams(collective_id=0, has_side_effects=True),
    )(x, q, w, lw)


def solution(mesh):
    depth = mesh.shape["seq"].bit_length() - 1
    rows = P(("groups", "seq"), None)
    return jax.shard_map(functools.partial(local, depth), mesh=mesh, in_specs=(rows, rows, P(), P()),
                         out_specs=rows, check_vma=False)
```

time: 98.2 us -> 45.9 us (0.47)
  matrix products: 49.8 us -> 0 us
  Pallas kernels: 0 us -> 41.2 us
  waiting for transfers between devices: 25.9 us -> 0 us
  starting transfers between devices: 7.88 us -> 0 us
  local copies, waits for them, and re-layouts: 9.83 us -> 4.43 us
  other arithmetic: 4.38 us -> 0 us
    dot_general x5 -> x0, matrix products: 49.8 us -> none  [the longest x1 17 us: local(): jnp.einsum('jih,ihab->jhab', coef, span_states, precision=highest)]
    pallas_call x0 -> x1, Pallas kernels: none -> 41.2 us  [local(): pl.pallas_call(functools.partial(kernel, depth, tokens, block, tile), out...]
    ppermute x4 -> x0, waiting for transfers between devices: 25.9 us -> none  [swapped(): lax.ppermute(x, axis, [(i, i ^ 1 << distance) for i in range(lax.axis_siz...]
    ppermute x4 -> x0, starting transfers between devices: 7.88 us -> none  [swapped(): lax.ppermute(x, axis, [(i, i ^ 1 << distance) for i in range(lax.axis_siz...]
    add x5 -> x0, other arithmetic: 3.7 us -> none  [the longest x3 2.08 us: remote_states(): block = block + partner]
    unnamed x11 -> x2, local copies, waits for them, and re-layouts: 7.94 us -> 4.43 us
    convert_element_type x1 -> x0, local copies, waits for them, and re-layouts: 1.77 us -> none  [local(): return (intra + inter).astype(jnp.bfloat16).reshape(tokens, width)]
  transfers between devices with their start and end apart: 4 -> 0, of which waited for: 3 -> 0; matrix products, arithmetic and copies ran while one was open for 28% -> 0% of each run, Pallas kernels for 0% -> 0%
where the time goes in v1:
time: 45.9 us; the launch traced here: 45.6 us
  Pallas kernels  41.2 us (90%)
  local copies, waits for them, and re-layouts  4.43 us (10%)
    pallas_call x1, Pallas kernels, local(): pl.pallas_call(functools.partial(kernel, depth, tokens, block, tile), out...  41.2 us
    unnamed x2, local copies, waits for them, and re-layouts  4.43 us

profile of v1, /device:TPU:0, one launch (start us, length us, event | category | flops | bytes accessed | tf_op | source)
XLA Modules:
  0.0 45.6 jit_solution(13489542291095472792)
XLA Ops:
  0.0 1.4 %copy.5.lw = f32[16,8]{1,0:T(8,128)} copy(f32[16,8]{0,1:T(8,128)} %param.7) | data formatting | bytes 1024 | tf_op args[3]
  1.4 41.2 %shard_map.46 = bf16[1024,1024]{1,0:T(8,128)(2,1)} custom-call(bf16[1024,2048]{1,0:T(8,128)(2,1)} %x_hbm.1, bf16[1024,1024]{1,0:T(8,128)(2,1)} %q_hbm.1, bf16[2048,2048]{1,0:T(8,128)(2,1)} %w_hbm.1, f32[16,8]{1,0:T(8,128)} %copy.5.lw), custom_call_target="tpu_custom_call" | custom-call | tf_op jit(solution)/shard_map/pallas_call | solution.py:209
  42.6 3.1 %copy.7 = bf16[1024,1024]{1,0:T(8,128)(2,1)} copy(bf16[1024,1024]{1,0:T(8,128)(2,1)} %shard_map.46) | data formatting | bytes 4194304

commit v2 on v1

--- a/solution.py
+++ b/solution.py
@@ -17,9 +17,9 @@
 BF16 = jnp.bfloat16
 
 
-def kernel(depth, tokens, block, tile, x_hbm, q_hbm, w_hbm, lw, out_hbm,
+def kernel(depth, tokens, block, tile, x_hbm, q_hbm, w_hbm, lw_hbm, out_hbm,
            x, w, q, kv, local, out, weight, states, total, near, away, sums, got,
-           x_sem, w_sem, q_sem, out_sem, near_send, near_recv, far_send, far_recv, share_send, share_recv):
+           lw, lw_sem, x_sem, w_sem, q_sem, out_sem, near_send, near_recv, far_send, far_recv, share_send, share_recv):
     width = HEADS * HEAD
     wide = PAIR * HEAD
     groups = HEADS // PAIR
@@ -49,6 +49,7 @@
         columns = pl.ds(g * wide, wide)
         return pltpu.make_async_copy(out.at[:, columns], out_hbm.at[:, columns], out_sem.at[g])
 
+    lw_copy = pltpu.make_async_copy(lw_hbm, lw, lw_sem)
     w_copy(0, 0).start()
     x_copy(0).start()
     w_copy(0, 1).start()
@@ -58,6 +59,7 @@
         w_copy(g, 0).start()
         w_copy(g, 1).start()
     q_copy.start()
+    lw_copy.start()
 
     def remote(src, dst, send, recv, partner):
         return pltpu.make_async_remote_copy(
@@ -74,8 +76,11 @@
     def share_copy(g):
         return remote(away.at[g, core], away.at[g, core], share_send.at[g], share_recv.at[g], partners[0])
 
+    def entry(row, head):
+        return lw[row:row + 1, head:head + 1]
+
     def factor(level, head):
-        return lw[1 + level, head] * (1.0 / math.sqrt(2**level * SPAN))
+        return entry(1 + level, head) * (1.0 / math.sqrt(2**level * SPAN))
 
     def project(g):
         kc = slice(g * wide, (g + 1) * wide)
@@ -99,6 +104,7 @@
                     states[g * PAIR + e, i * (tile // block) + b] = both[own, own]
 
         if g == 0:
+            lw_copy.wait()
             for i in range(tiles):
                 x_copy(i).wait()
                 body(i)
@@ -115,14 +121,13 @@
         differ = (target // SPAN) ^ (source // SPAN)
         for e in range(PAIR):
             head = g * PAIR + e
-            at = jnp.full((block, block), lw[0, head] * (1.0 / math.sqrt(SPAN * HEAD)), F32)
+            at = jnp.broadcast_to(entry(0, head) * (1.0 / math.sqrt(SPAN * HEAD)), (block, block))
             for level in range(inner_bits):
                 at = jnp.where(differ >= 1 << level, factor(level, head) * (1.0 / math.sqrt(HEAD)), at)
             weight[e] = jnp.where(source <= target, at, 0.0)
 
-        @pl.loop(0, blocks)
-        def _(b):
-            rows = pl.ds(pl.multiple_of(b * block, block), block)
+        for b in range(blocks):
+            rows = slice(b * block, (b + 1) * block)
             for e in range(PAIR):
                 head = g * PAIR + e
                 columns = slice(head * HEAD, (head + 1) * HEAD)
@@ -170,7 +175,8 @@
             level = s - 1
             far_copy(g, level).wait()
             bit = (jnp.right_shift(index, level) & 1).astype(F32)
-            term = (bit * factor(local_bits + level, g * PAIR + core)) * got[level - 1, g]
+            scale = jnp.where(core == 0, factor(local_bits + level, g * PAIR), factor(local_bits + level, g * PAIR + 1))
+            term = (bit * scale) * got[level - 1, g]
             away[g, core] = term if level == 1 else away[g, core] + term
             if level + 1 < depth:
                 sums[level, g] = sums[level - 1, g] + got[level - 1, g]
@@ -181,18 +187,19 @@
             share_copy(g).wait()
             finish(g)
 
-    for slot in range(2 * groups + depth + 1):
+    last = max(depth + 4, 2 * groups)
+    for slot in range(groups + last):
         if slot < groups:
             project(slot)
         elif slot < 2 * groups:
             attend(slot - groups)
-        for g in range(groups):
+        for g in reversed(range(groups)):
             lag = slot - g
-            if slot >= groups and g == groups - 1:
-                lag = slot - g
-            if 0 <= lag <= depth:
+            if 0 <= lag < depth:
                 stage(g, lag)
-            if slot >= 2 * groups - 1 and lag == max(depth + 1, 2 * groups - 1 - g):
+            elif lag == depth + 2:
+                stage(g, depth)
+            elif lag == last:
                 stage(g, depth + 1)
     for g in range(groups):
         out_copy(g).wait()
@@ -202,14 +209,14 @@
     tokens, width = q.shape
     groups = HEADS // PAIR
     block = min(256, tokens)
-    tile = min(512, tokens)
+    tile = min(1024, tokens)
     levels = max(depth - 1, 1)
     dma = pltpu.SemaphoreType.DMA
     hbm = pl.BlockSpec(memory_space=pl.ANY)
     return pl.pallas_call(
         functools.partial(kernel, depth, tokens, block, tile),
         out_shape=jax.ShapeDtypeStruct((tokens, width), BF16),
-        in_specs=[hbm, hbm, hbm, pl.BlockSpec(memory_space=pltpu.SMEM)],
+        in_specs=[hbm, hbm, hbm, hbm],
         out_specs=hbm,
         scratch_shapes=[
             pltpu.VMEM(x.shape, BF16),
@@ -225,7 +232,8 @@
             pltpu.VMEM((groups, PAIR, HEAD, HEAD), F32),
             pltpu.VMEM((levels, groups, HEAD, HEAD), F32),
             pltpu.VMEM((levels, groups, HEAD, HEAD), F32),
-            dma((tokens // tile,)), dma((groups, 2)), dma, dma((groups,)),
+            pltpu.VMEM(lw.shape, F32),
+            dma, dma((tokens // tile,)), dma((groups, 2)), dma, dma((groups,)),
             dma((groups,)), dma((groups,)), dma((levels, groups)), dma((levels, groups)),
             dma((groups,)), dma((groups,)),
         ],

time: 45.9 us -> 40.8 us (0.89)
  Pallas kernels: 41.2 us -> 36.1 us
    pallas_call x1, Pallas kernels: 41.2 us -> 36.1 us  [local(): pl.pallas_call(functools.partial(kernel, depth, tokens, block, tile), out...]
where the time goes in v2:
time: 40.8 us; the launch traced here: 40.5 us
  Pallas kernels  36.1 us (88%)
  local copies, waits for them, and re-layouts  4.43 us (11%)
    pallas_call x1, Pallas kernels, local(): pl.pallas_call(functools.partial(kernel, depth, tokens, block, tile), out...  36.1 us
    unnamed x2, local copies, waits for them, and re-layouts  4.43 us

profile of v2, /device:TPU:0, one launch (start us, length us, event | category | flops | bytes accessed | tf_op | source)
XLA Modules:
  0.0 40.5 jit_solution(9243305848622094791)
XLA Ops:
  0.0 1.4 %copy.5.lw_hbm = f32[16,8]{1,0:T(8,128)} copy(f32[16,8]{0,1:T(8,128)} %param.7) | data formatting | bytes 1024 | tf_op args[3]
  1.4 36.1 %shard_map.46 = bf16[1024,1024]{1,0:T(8,128)(2,1)} custom-call(bf16[1024,2048]{1,0:T(8,128)(2,1)} %x_hbm.1, bf16[1024,1024]{1,0:T(8,128)(2,1)} %q_hbm.1, bf16[2048,2048]{1,0:T(8,128)(2,1)} %w_hbm.1, f32[16,8]{1,0:T(8,128)} %copy.5.lw_hbm), custom_call_target="tpu_custom_call" | custom-call | tf_op jit(solution)/shard_map/pallas_call | solution.py:216
  37.4 3.1 %copy.7 = bf16[1024,1024]{1,0:T(8,128)(2,1)} copy(bf16[1024,1024]{1,0:T(8,128)(2,1)} %shard_map.46) | data formatting | bytes 4194304
